TPU v7x, 128 devices: a whole 4x4x4 slice. The times are simulated.
128 devices in a mesh: gx: 4 (over y), gy: 32 (over z, x, core).
Axes of the slice: x: 4, y: 4, z: 4, core: 2. Of those that a mesh axis runs over, the one named last changes fastest.
Arguments:
- background: float32 [256, 4, 512, 512], P(('gx', 'gy')), may hold values from -6 to 6
- obs_cells: int32 [32, 32, 1024], P('gy', 'gx'), may hold values from 0 to 2303
- obs_counts: int32 [32, 32], P('gy', 'gx'), may hold values from 1 to 1024, as said below
- obs_widths: int32 [32, 32], P('gy', 'gx'), may hold values from 1 to 4
- obs_values: float32 [32, 32, 1024], P('gy', 'gx'), may hold values from -6 to 6
- obs_variances: float32 [32, 32, 1024], P('gy', 'gx'), may hold values from 1 to 16
Outputs:
- analysis: float32 [256, 4, 512, 512], P(('gx', 'gy'))
Inputs may be any that keep to these rules, and one draw needn't show every extreme that they name: `obs_cells`: each is level * 24 * 24 + row * 24 + column of a cell in the patch's surrounding region. `obs_counts`: some patch uses all 1024 slots.
All inputs are finite; a program needn't handle non-finite values.
Results may differ from a plain program's by a relative error of at most 0.0003.
Values sent between devices are 32-bit elements; how exact they have to be, the bound alone decides.
No kernel may reach another device: no remote copies, remote signals or barrier semaphores. Data moves between devices by JAX's collectives and lax.ppermute only.
A program may use at most 256 MiB of HBM per device.

v0:
```python
import functools

import jax
import jax.numpy as jnp
from jax import lax
from jax.experimental import pallas as pl
from jax.experimental.pallas import tpu as pltpu
from jax.sharding import PartitionSpec as P

F32 = jnp.float32
BF16 = jnp.bfloat16
ITERS = 5
FIRST, SECOND = (1, 3), (5, 7)


def lane_group(shape):
    return lax.broadcasted_iota(jnp.int32, shape, len(shape) - 1) // 16


def skew(tiles):
    group = lane_group(tiles[0].shape)
    for bit in (1, 2, 4):
        odd = (group & bit) != 0
        tiles = [jnp.where(odd, tiles[(k + bit) % 8], tiles[k]) for k in range(8)]
    return tiles


def edge_lanes():
    shape = (8, 128)
    low = lax.broadcasted_iota(jnp.int32, shape, 0) < 4
    return (lane_group(shape) % 2 == 0) == low


def pack_kernel(x_ref, o_ref, *, edge):
    first = edge_lanes()

    @pl.loop(0, o_ref.shape[1])
    def _(band):
        for member in range(2):
            for col in range(4):
                tiles = []
                for t in range(8):
                    rows = pl.ds(pl.multiple_of(16 * band + 8 * (t % 2), 8), 8)
                    tile = x_ref[member, t // 2, rows, 128 * col : 128 * col + 128]
                    tiles.append(pltpu.roll(tile, 16 * t, 1) if t else tile)
                tiles = skew(tiles)
                for i in range(4):
                    even, odd = tiles[(8 - 2 * i) % 8], tiles[7 - 2 * i]
                    merged = jnp.where(first, even, odd) if edge else jnp.where(first, odd, even)
                    o_ref[col, band, member, 8 * i : 8 * i + 8, :] = merged


def pack(x, edge, bands=8):
    return pl.pallas_call(
        functools.partial(pack_kernel, edge=edge),
        grid=(32 // bands,),
        in_specs=[pl.BlockSpec((2, 4, 16 * bands, 512), lambda i: (0, 0, i, 0))],
        out_specs=pl.BlockSpec((4, bands, 2, 32, 128), lambda i: (0, i, 0, 0, 0)),
        out_shape=jax.ShapeDtypeStruct((4, 32, 2, 32, 128), F32),
        cost_estimate=pl.CostEstimate(flops=10**10, bytes_accessed=12 * 2**20, transcendentals=0),
        name="pack_edge" if edge else "pack_inner",
    )(x)


def unpack_kernel(a_ref, b_ref, o_ref, *, order):
    place = {p: (a_ref, i) for i, p in enumerate(order[0])}
    place.update({p: (b_ref, i) for i, p in enumerate(order[1])})

    @pl.loop(0, a_ref.shape[1])
    def _(band):
        for member in range(2):
            for col in range(4):
                tiles = []
                for p in range(8):
                    ref, i = place[p]
                    tiles.append(ref[col, band, member, 8 * i : 8 * i + 8, :])
                tiles = skew(tiles)
                for t in range(8):
                    tile = tiles[(8 - t) % 8]
                    tile = pltpu.roll(tile, 128 - 16 * t, 1) if t else tile
                    rows = pl.ds(pl.multiple_of(16 * band + 8 * (t % 2), 8), 8)
                    o_ref[member, t // 2, rows, 128 * col : 128 * col + 128] = tile


def unpack(a, b, order, bands=8):
    na, nb = 8 * len(order[0]), 8 * len(order[1])
    return pl.pallas_call(
        functools.partial(unpack_kernel, order=order),
        grid=(32 // bands,),
        in_specs=[
            pl.BlockSpec((4, bands, 2, na, 128), lambda i: (0, i, 0, 0, 0)),
            pl.BlockSpec((4, bands, 2, nb, 128), lambda i: (0, i, 0, 0, 0)),
        ],
        out_specs=pl.BlockSpec((2, 4, 16 * bands, 512), lambda i: (0, 0, i, 0)),
        out_shape=jax.ShapeDtypeStruct((2, 4, 512, 512), F32),
        name="unpack",
    )(a, b)


def three_way(x):
    high = x.astype(BF16)
    rest = x - high.astype(F32)
    mid = rest.astype(BF16)
    return high, mid, (rest - mid.astype(F32)).astype(BF16)


def two_way(x):
    high = x.astype(BF16)
    return high, (x - high.astype(F32)).astype(BF16)


def cells_kernel(kc_ref, lane_ref, w_ref, v_ref, o_ref):
    kc = kc_ref[0]
    slots = kc.shape[1]
    row_hit = lax.broadcasted_iota(jnp.int32, (24, slots), 0) == kc
    lane_hit = lax.broadcasted_iota(jnp.int32, (128, slots), 0) == lane_ref[0]
    lane_hot = jnp.where(lane_hit, 1.0, 0.0).astype(BF16)
    both = jnp.concatenate(
        [jnp.where(row_hit, w_ref[0], 0.0), jnp.where(row_hit, v_ref[0], 0.0)], axis=0
    )
    total = jnp.zeros((48, 128), F32)
    for part in three_way(both):
        total = total + lax.dot_general(
            part, lane_hot, (((1,), (1,)), ((), ())), preferred_element_type=F32
        )
    w = total[:24]
    root = jnp.where(w > 0.0, jnp.sqrt(jnp.maximum(w, 1e-30)), 0.0)
    o_ref[0] = jnp.concatenate([total, root], axis=0)


def cell_sums(obs_cells, obs_counts, obs_widths, obs_values, obs_variances):
    number, slots = obs_cells.shape
    level = obs_cells // 576
    row = obs_cells // 24 % 24
    col = obs_cells % 24
    row_out = jnp.maximum(jnp.maximum(4 - row, row - 19), 0)
    col_out = jnp.maximum(jnp.maximum(4 - col, col - 19), 0)
    distance = jnp.maximum(row_out, col_out)
    slot = lax.broadcasted_iota(jnp.int32, obs_cells.shape, 1)
    usable = (slot < obs_counts[:, None]) & (distance <= obs_widths[:, None])
    relative = distance.astype(F32) / (obs_widths[:, None] + 1).astype(F32)
    w = jnp.where(usable, jnp.exp(-relative * relative) / obs_variances, 0.0)
    v = w * obs_values
    t = 2 * level + jnp.where((row >= 12) & (row < 20) | (row < 4), 1, 0)
    halo = (row < 4) | (row >= 20)
    inside = (row >= 8) & (row < 16)
    west, east = col < 4, col >= 20
    shift = jnp.where(west, -1, jnp.where(east, 1, 0))
    inner = jnp.where(west, 12 + col, jnp.where(east, col - 20, col - 4))
    p = lax.broadcasted_iota(jnp.int32, obs_cells.shape, 0)
    lane = 16 * ((t + p + shift + 8) % 8) + inner
    side = jnp.where(west | east, 1, 0)
    kc = row % 4 + jnp.where(inside, 16 + 4 * side, 8 * side + jnp.where(halo, 4, 0))
    spec = pl.BlockSpec((1, 1, slots), lambda i: (i, 0, 0))
    shape = (number, 1, slots)
    return pl.pallas_call(
        cells_kernel,
        grid=(number,),
        in_specs=[spec] * 4,
        out_specs=pl.BlockSpec((1, 72, 128), lambda i: (i, 0, 0)),
        out_shape=jax.ShapeDtypeStruct((number, 72, 128), F32),
        cost_estimate=pl.CostEstimate(flops=5 * 10**9, bytes_accessed=2**20, transcendentals=0),
        name="cells",
    )(kc.reshape(shape), lane.reshape(shape), w.reshape(shape), v.reshape(shape))


def take(ref, row):
    members, rows, lanes = ref.shape
    return ref.reshape(members * rows, lanes)[pl.ds(row, members, stride=rows), :]


def put(ref, row, value):
    members, rows, lanes = ref.shape
    ref.reshape(members * rows, lanes)[pl.ds(row, members, stride=rows), :] = value


def odd_rows(odd):
    return ((lane_group((1, 128)) - odd) & 1) == 1


def column(kind, q, patch, above, below):
    edge, inner, pair, odd = patch
    if kind == "edge":
        a, b = take(edge, q), take(edge, 4 + q)
    elif kind == "inner":
        a, b = take(inner, 4 + q), take(inner, q)
    else:
        a, b = take(below, 4 * pair + q), take(above, 4 * pair + q)
    return jnp.where(odd_rows(odd), b, a)


def sides_kernel(*refs, kinds):
    count = len(kinds)
    first_ref, last_ref = refs[:2]
    above, below = refs[2:4] if "halo" in kinds else (None, None)
    left_ref, right_ref = refs[-2:]
    within = lax.broadcasted_iota(jnp.int32, (1, 128), 1) % 16 // 4
    for j in range(count):
        left = right = None
        for i in range(4):
            f = column(kinds[j], i, (first_ref, first_ref, 0, 0), above, below)
            f = pltpu.roll(f, 4 * i, 1) if i else f
            l = column(kinds[j], i, (last_ref, last_ref, 3, 1), above, below)
            l = pltpu.roll(l, 128 - 4 * (3 - i), 1) if i < 3 else l
            left = f if left is None else jnp.where(within == i, f, left)
            right = l if right is None else jnp.where(within == i, l, right)
        left_ref[:, 128 * j : 128 * j + 128] = left
        right_ref[:, 128 * j : 128 * j + 128] = right


def whole(shape):
    return pl.BlockSpec(shape, lambda i: (0,) * len(shape))


def sides(x, kinds, *halo):
    width = 128 * len(kinds)
    return pl.pallas_call(
        functools.partial(sides_kernel, kinds=kinds),
        grid=(1,),
        in_specs=[
            pl.BlockSpec((256, 8, 128), lambda i: (0, 0, 0)),
            pl.BlockSpec((256, 8, 128), lambda i: (0, 3, 0)),
        ]
        + [whole((256, 16, 128))] * len(halo),
        out_specs=[whole((256, width))] * 2,
        out_shape=[jax.ShapeDtypeStruct((256, width), F32)] * 2,
        cost_estimate=pl.CostEstimate(flops=10**9, bytes_accessed=4 * 2**20, transcendentals=0),
        name="sides",
    )(x, x, *halo)


def dot(a, b):
    return jnp.dot(a, b, preferred_element_type=F32)


def product(a, b):
    (ah, al), (bh, bl) = a, b
    return dot(jnp.concatenate([ah, ah, al], axis=1), jnp.concatenate([bh, bl, bh], axis=0))


def gram_of(kinds, base, west, mine, east, above, below, far, wv, high_ref, low_ref, gram_ref):
    total = jnp.zeros((256, 128), F32)
    within = lax.broadcasted_iota(jnp.int32, (1, 128), 1) % 16
    place = 0
    for strip in (False, True):
        for j, kind in enumerate(kinds):
            for q in range(4):
                if not strip:
                    x = column(kind, q, mine, above, below)
                else:
                    l = column(kind, q, west, above, below)
                    r = column(kind, q, east, above, below)
                    if far is not None:
                        ref, from_west, outer = far
                        v = ref[:, 128 * j : 128 * j + 128]
                        if from_west:
                            v = pltpu.roll(v, 4 * (3 - q), 1) if q < 3 else v
                            l = jnp.where(outer, v, l)
                        else:
                            v = pltpu.roll(v, 128 - 4 * q, 1) if q else v
                            r = jnp.where(outer, v, r)
                    x = jnp.where(within < 8, r, l)
                c = base + place
                w = wv[0, c : c + 1, :]
                v = wv[0, 24 + c : 25 + c, :]
                root = wv[0, 48 + c : 49 + c, :]
                mean = jnp.sum(x, axis=0, keepdims=True) * (1.0 / 256)
                dev = x - mean
                total = total + dev * (v - w * mean)
                high, low = two_way(dev * root)
                high_ref[:, 128 * place : 128 * place + 128] = high
                low_ref[:, 128 * place : 128 * place + 128] = low
                place += 1
    nt = (((1,), (1,)), ((), ()))
    high, low = high_ref[:, : 128 * place], low_ref[:, : 128 * place]
    gram_ref[0] = lax.dot_general(high, high, nt, preferred_element_type=F32)
    gram_ref[1] = lax.dot_general(high, low, nt, preferred_element_type=F32)
    cross = gram_ref[1]
    return gram_ref[0] + (cross + cross.T), total


def early_kernel(start, *refs):
    e0, e1, above, below, wv0, wv1 = refs[:6]
    gram_out, pulled_out, h0, l0, h1, l1, g0, g1 = refs[-8:]
    pair = start + pl.program_id(0)
    patches = [(e, None, (pair + i // 2) % 4, i % 2) for i, e in enumerate((e0, e0, e1, e1))]
    fars = [(refs[7], False, True), (refs[6], True, True)] if start == 3 else [None, None]
    for k, wv, h, l, g in ((0, wv0, h0, l0, g0), (1, wv1, h1, l1, g1)):
        gram, total = gram_of(
            ("edge", "halo"), 0, *patches[k : k + 3], above, below, fars[k], wv, h, l, g
        )
        gram_out[k] = gram
        pulled_out[k] = total


def early(edge, above, below, wv, start, steps, *last):
    args = [edge, edge, above, below, wv, wv, *last]
    specs = [
        pl.BlockSpec((256, 8, 128), lambda i: (0, start + i, 0)),
        pl.BlockSpec((256, 8, 128), lambda i: (0, (start + i + 1) % 4, 0)),
        whole((256, 16, 128)),
        whole((256, 16, 128)),
        pl.BlockSpec((1, 72, 128), lambda i: (2 * (start + i) + 1, 0, 0)),
        pl.BlockSpec((1, 72, 128), lambda i: ((2 * (start + i) + 2) % 8, 0, 0)),
    ]
    if last:
        specs += [whole((256, 256))] * 2 + [pl.BlockSpec(memory_space=pl.ANY)] * 2
    return pl.pallas_call(
        functools.partial(early_kernel, start),
        grid=(steps,),
        in_specs=specs,
        out_specs=[
            pl.BlockSpec((2, 256, 256), lambda i: (start + i, 0, 0)),
            pl.BlockSpec((2, 256, 128), lambda i: (start + i, 0, 0)),
        ],
        out_shape=[
            jax.ShapeDtypeStruct((8, 256, 256), F32),
            jax.ShapeDtypeStruct((8, 256, 128), F32),
        ],
        input_output_aliases={8: 0, 9: 1} if last else {},
        scratch_shapes=[pltpu.VMEM((256, 2048), BF16)] * 4 + [pltpu.VMEM((2, 256, 256), F32)] * 2,
        compiler_params=pltpu.CompilerParams(vmem_limit_bytes=58 * 1024 * 1024),
        cost_estimate=pl.CostEstimate(
            flops=steps * 7 * 10**9, bytes_accessed=steps * 4 * 2**20, transcendentals=0
        ),
        name="early",
    )(*args)


def newton(s0, s1, last):
    row = lax.broadcasted_iota(jnp.int32, (256, 256), 0)
    col = lax.broadcasted_iota(jnp.int32, (256, 256), 1)
    eye = jnp.where(row == col, 1.5, 0.0)
    halves = [(two_way(s[0]), two_way(s[1])) for s in (s0, s1)]
    both = [product(inv, cur) for cur, inv in halves]
    factors = [two_way(eye - 0.5 * x) for x in both]
    if not last:
        for s, (cur, _), factor in zip((s0, s1), halves, factors):
            s[0] = product(cur, factor)
    for s, (_, inv), factor in zip((s0, s1), halves, factors):
        s[1] = product(factor, inv)


def start_newton(gram, s):
    squares = jnp.sum(jnp.sum(gram * gram, axis=0, keepdims=True), axis=1, keepdims=True)
    divisor = 255.0 + jnp.sqrt(jnp.maximum(squares, 1e-30))
    row = lax.broadcasted_iota(jnp.int32, (256, 256), 0)
    col = lax.broadcasted_iota(jnp.int32, (256, 256), 1)
    eye = row == col
    current = (gram + jnp.where(eye, 255.0, 0.0)) / divisor
    inverse = jnp.where(eye, 1.5, 0.0) - 0.5 * current
    s[0] = product(two_way(current), two_way(inverse))
    s[1] = inverse
    return divisor


def apply(inverse, pulled, divisor, mine, out, base):
    halfway = jnp.sum(inverse * pulled, axis=0, keepdims=True)
    weight = jnp.sum(inverse * halfway, axis=1, keepdims=True) / divisor
    zh, zl = two_way(inverse * jnp.sqrt(255.0 / divisor))
    z = jnp.concatenate([zh, zh, zl], axis=1)
    edge, inner, _, odd = mine
    for q in range(0, 8, 2):
        parts, bases = [], []
        for k in range(2):
            a, b = take(edge, q + k), take(inner, q + k)
            x = jnp.where(odd_rows(odd), b, a) if q < 4 else jnp.where(odd_rows(odd), a, b)
            centre = jnp.sum(x, axis=0, keepdims=True) * (1.0 / 256)
            dev = x - centre
            bases.append(centre + jnp.sum(dev * weight, axis=0, keepdims=True))
            parts.append(dev)
        dh, dl = two_way(jnp.concatenate(parts, axis=1))
        mixed = dot(z, jnp.concatenate([dh, dl, dh], axis=0))
        for k in range(2):
            put(out, base + q + k, mixed[:, 128 * k : 128 * k + 128] + bases[k])


def analysis_kernel(pairs, outer, *refs):
    e0, e1, i0, i1, gram_in, pulled_in, wv0, wv1 = refs[:8]
    refs = refs[8:]
    step = pl.program_id(0)
    pair = (pairs[0] - 1) // 2 + step
    fars = [None, None]
    if outer:
        fars = [(refs[1], False, pair == 3), (refs[0], True, pair == 3)]
        refs = refs[2:]
    out, h0, l0, h1, l1, g0, g1, s0, s1 = refs
    patches = [
        (e, n, (pair + i // 2) % 4, i % 2) for i, (e, n) in enumerate(((e0, i0),) * 2 + ((e1, i1),) * 2)
    ]
    pulled, divisors = [], []
    for k, wv, h, l, g, s in ((0, wv0, h0, l0, g0, s0), (1, wv1, h1, l1, g1, s1)):
        gram, total = gram_of(("inner",), 16, *patches[k : k + 3], None, None, fars[k], wv, h, l, g)
        pulled.append(jnp.sum(total + pulled_in[k], axis=1, keepdims=True))
        divisors.append(start_newton(gram + gram_in[k], s))

    def body(_, carry):
        newton(s0, s1, False)
        return carry

    lax.fori_loop(0, ITERS - 2, body, 0)
    newton(s0, s1, True)
    for k, s in ((0, s0), (1, s1)):
        apply(s[1], pulled[k], divisors[k], patches[k + 1], out, 8 * k)


def analysis(edge, inner, grams, pulls, wv, pairs, *ends):
    outer = pairs[-1] == 7
    steps = len(pairs)
    start = (pairs[0] - 1) // 2

    def block(shift):
        return pl.BlockSpec((256, 8, 128), lambda i: (0, (start + i + shift) % 4, 0))

    def cells(shift):
        return pl.BlockSpec((1, 72, 128), lambda i: ((2 * (start + i) + 1 + shift) % 8, 0, 0))

    def held(width):
        return pl.BlockSpec((2, 256, width), lambda i: (start + i, 0, 0))

    args = [edge, edge, inner, inner, grams, pulls, wv, wv]
    specs = [block(0), block(1), block(0), block(1), held(256), held(128), cells(0), cells(1)]
    if outer:
        args += list(ends)
        specs += [whole(v.shape) for v in ends]
    return pl.pallas_call(
        functools.partial(analysis_kernel, pairs, outer),
        grid=(steps,),
        in_specs=specs,
        out_specs=pl.BlockSpec((256, 16, 128), lambda i: (0, i, 0)),
        out_shape=jax.ShapeDtypeStruct((256, 16 * steps, 128), F32),
        scratch_shapes=[pltpu.VMEM((256, 1024), BF16)] * 4 + [pltpu.VMEM((2, 256, 256), F32)] * 4,
        compiler_params=pltpu.CompilerParams(vmem_limit_bytes=58 * 1024 * 1024),
        cost_estimate=pl.CostEstimate(
            flops=steps * 12 * 10**9, bytes_accessed=steps * 6 * 2**20, transcendentals=0
        ),
        name="analysis",
    )(*args)


def shards(background, obs_cells, obs_counts, obs_widths, obs_values, obs_variances):
    axes = ("gx", "gy")
    gx, gy = lax.axis_size("gx"), lax.axis_size("gy")
    onward = [(i, i + 1) for i in range(gy - 1)]
    ring = [(i, (i + 1) % gx) for i in range(gx)]

    def exchange(x):
        return lax.all_to_all(x, axes, split_axis=0, concat_axis=0, tiled=True)

    def beside(pair):
        to_left, to_right = pair
        left = lax.ppermute(to_right, "gx", ring)
        return left, lax.ppermute(to_left, "gx", [(j, i) for i, j in ring])

    edge = exchange(pack(background, True).reshape(256, 32, 128))
    send = pack(background, False).reshape(256, 32, 128)
    wv = cell_sums(obs_cells[0], obs_counts[0], obs_widths[0], obs_values[0], obs_variances[0])
    tiles = edge.reshape(256, 4, 8, 128)
    up = tiles[:, :, 0:4].reshape(256, 16, 128)
    dn = tiles[:, :, 4:8].reshape(256, 16, 128)
    up, dn = lax.optimization_barrier((up, dn))
    above = lax.ppermute(dn, "gy", onward)
    below = lax.ppermute(up, "gy", [(j, i) for i, j in onward])
    inner = exchange(send)
    sides_e = beside(sides(edge, ("edge", "halo"), above, below))
    partial = early(edge, above, below, wv, 0, 3)
    sides_i = beside(sides(inner, ("inner",)))
    out = analysis(edge, inner, *partial, wv, FIRST)
    out, sides_e, sides_i = lax.optimization_barrier((out, sides_e, sides_i))
    results = [exchange(out)]
    partial = early(edge, above, below, wv, 3, 1, *sides_e, *partial)
    out = analysis(edge, inner, *partial, wv, SECOND, *sides_i)
    results.append(exchange(out))
    order = [[q % 8 for p in pairs for q in (p, p + 1)] for pairs in (FIRST, SECOND)]
    a, b = [r.reshape(4, 32, 2, r.shape[1], 128) for r in results]
    return unpack(a, b, order)


def solution(mesh):
    return jax.shard_map(
        shards,
        mesh=mesh,
        in_specs=(
            P(("gx", "gy"), None, None, None),
            P("gy", "gx", None),
            P("gy", "gx"),
            P("gy", "gx"),
            P("gy", "gx", None),
            P("gy", "gx", None),
        ),
        out_specs=P(("gx", "gy"), None, None, None),
        check_vma=False,
    )
```

profile of v0, /device:TPU:1, one launch (start us, length us, event | category | flops | bytes accessed | tf_op | source)
XLA Modules:
  0.0 368.4 jit_solution(7296723450188704964)
XLA Ops:
  0.0 7.9 %pack_edge.1 = f32[4,32,2,32,128]{4,3,2,1,0:T(8,128)} custom-call(f32[2,4,512,512]{3,2,1,0:T(8,128)} %x_ref.3), custom_call_target="tpu_custom_call" | custom-call | flops 10000000000 | bytes 12582912 | tf_op jit(solution)/shard_map/pack_edge/pallas_call | solution.py:54
  7.9 11.9 %all-to-all-start = ((f32[256,32,128]{2,1,0:T(8,128)}), f32[256,32,128]{2,1,0:T(8,128)}, u32[]{:S(2)}, u32[]{:S(2)}) async-start(f32[256,32,128]{2,1,0:T(8,128)} %bitcast.38), calls=%async_computation | async-start | bytes 8388608 | tf_op jit(solution)/shard_map/all_to_all | solution.py:448
  19.9 7.9 %pack_inner.1 = f32[4,32,2,32,128]{4,3,2,1,0:T(8,128)} custom-call(f32[2,4,512,512]{3,2,1,0:T(8,128)} %x_ref.3), custom_call_target="tpu_custom_call" | custom-call | flops 10000000000 | bytes 12582912 | tf_op jit(solution)/shard_map/pack_inner/pallas_call | solution.py:54
  27.8 44.7 %all-to-all-done.refs_0_.refs_1_ = f32[256,32,128]{2,1,0:T(8,128)} async-done(((f32[256,32,128]{2,1,0:T(8,128)}), f32[256,32,128]{2,1,0:T(8,128)}, u32[]{:S(2)}, u32[]{:S(2)}) %all-to-all-start) | async-done | bytes 4194336 | tf_op jit(solution)/shard_map/all_to_all | solution.py:448
  72.4 5.5 %all-to-all-start.1 = ((f32[256,32,128]{2,1,0:T(8,128)}), f32[256,32,128]{2,1,0:T(8,128)}, u32[]{:S(2)}, u32[]{:S(2)}) async-start(f32[256,32,128]{2,1,0:T(8,128)} %bitcast.37), calls=%async_computation.1 | async-start | bytes 8388608 | tf_op jit(solution)/shard_map/all_to_all | solution.py:448
  78.0 0.0 copy-start.5
  78.0 0.0 copy-start.2
  78.0 0.0 copy-start.3
  78.0 0.0 copy-start.4
  78.0 0.0 copy-start.6
  78.0 6.5 %fusion.13 = (f32[256,4,4,128]{3,2,1,0:T(4,128)}, f32[256,4,4,128]{3,2,1,0:T(4,128)}) fusion(f32[256,4,8,128]{3,2,1,0:T(8,128)} %bitcast.2), kind=kLoop, calls=%fused_computation.39 | loop fusion | bytes 8388608 | tf_op jit(solution)/shard_map/slice | solution.py:460
  84.6 3.5 collective-permute-start
  88.1 1.9 collective-permute-start.1
  90.0 0.0 copy-done.5
  90.1 0.0 copy-done.2
  90.1 0.1 remainder_compare_fusion
  90.2 0.1 bitcast_and_fusion
  90.3 0.0 copy-done.3
  90.3 0.0 copy-done.4
  90.3 0.0 copy-done.6
  90.4 0.9 reshape_multiply_fusion
  91.3 1.3 fusion.8
  92.6 5.7 %cells.1.refs_4_.refs_5_.refs_6_.refs_7_ = f32[8,72,128]{2,1,0:T(8,128)} custom-call(s32[8,1,1024]{2,1,0:T(1,128)} %get-tuple-element.43.kc_ref, s32[8,1,1024]{2,1,0:T(1,128)} %get-tuple-element.42.lane_ref, f32[8,1,1024]{2,1,0:T(1,128)} %get-tuple-element.36.w_ref, f32[8,1,1024]{2,1,0:T(1,128)} %get-tuple-element.35.v_ref), custom_call_target="tpu_custom_call" | custom-call | flops 5000000000 | bytes 1048576 | tf_op jit(solution)/shard_map/cells/pallas_call | solution.py:156
  98.2 32.4 %all-to-all-done.1.refs_2_.refs_3_.refs_0_.refs_1_ = f32[256,32,128]{2,1,0:T(8,128)} async-done(((f32[256,32,128]{2,1,0:T(8,128)}), f32[256,32,128]{2,1,0:T(8,128)}, u32[]{:S(2)}, u32[]{:S(2)}) %all-to-all-start.1) | async-done | bytes 4194336 | tf_op jit(solution)/shard_map/all_to_all | solution.py:448
  130.7 2.5 sides.3
  133.2 0.0 collective-permute-start.4
  133.2 2.7 collective-permute-start.5
  135.9 9.0 %collective-permute-done.refs_2_ = f32[256,16,128]{2,1,0:T(8,128)S(1)} collective-permute-done((f32[256,16,128]{2,1,0:T(8,128)}, f32[256,16,128]{2,1,0:T(8,128)S(1)}, u32[]{:S(2)}, u32[]{:S(2)}) %collective-permute-start) | collective-permute-done | bytes 2097184 | tf_op jit(solution)/shard_map/ppermute | solution.py:462
  144.9 0.0 copy-start.1
  144.9 1.8 collective-permute-done.1.refs_3_
  146.7 0.0 copy-done.1
  146.7 4.9 %sides.2 = (f32[256,256]{1,0:T(8,128)}, f32[256,256]{1,0:T(8,128)}) custom-call(f32[256,32,128]{2,1,0:T(8,128)} %all-to-all-done.refs_0_.refs_1_, f32[256,32,128]{2,1,0:T(8,128)} %all-to-all-done.refs_0_.refs_1_, f32[256,16,128]{2,1,0:T(8,128)} %copy-done.1, f32[256,16,128]{2,1,0:T(8,128)} %collective-permute-done.1.refs_3_), custom_call_target="tpu_custom_call" | custom-call | flops 1000000000 | bytes 4194304 | tf_op jit(solution)/shard_map/sides/pallas_call | solution.py:217
  151.6 1.4 collective-permute-start.2
  153.0 1.3 collective-permute-start.3
  154.4 27.1 %early.2 = (f32[8,256,256]{2,1,0:T(8,128)}, f32[8,256,128]{2,1,0:T(8,128)}) custom-call(f32[256,32,128]{2,1,0:T(8,128)} %all-to-all-done.refs_0_.refs_1_, f32[256,32,128]{2,1,0:T(8,128)} %all-to-all-done.refs_0_.refs_1_, f32[256,16,128]{2,1,0:T(8,128)} %copy-done.1, f32[256,16,128]{2,1,0:T(8,128)} %collective-permute-done.1.refs_3_, ...), custom_call_target="tpu_custom_call" | custom-call | flops 20999999488 | bytes 12582912 | tf_op jit(solution)/shard_map/early/pallas_call | solution.py:308
  181.5 23.1 %analysis.2 = f32[256,32,128]{2,1,0:T(8,128)} custom-call(f32[256,32,128]{2,1,0:T(8,128)} %all-to-all-done.refs_0_.refs_1_, f32[256,32,128]{2,1,0:T(8,128)} %all-to-all-done.refs_0_.refs_1_, f32[256,32,128]{2,1,0:T(8,128)} %all-to-all-done.1.refs_2_.refs_3_.refs_0_.refs_1_, f32[256,32,128]{2,1,0:T(8,128)} %all-to-all-done.1.refs_2_.refs_3_.refs_0_.refs_1_, ...), custom_call_target="tpu_custom_call" | custom-call | flops 24000000000 | bytes 12582912 | tf_op jit(solution)/shard_map/analysis/pallas_call | solution.py:426
  204.6 0.0 collective-permute-done.4.refs_8_
  204.6 0.0 copy-start.9
  204.6 0.0 collective-permute-done.5.refs_9_
  204.6 0.0 copy-start.10
  204.6 0.0 collective-permute-done.2.refs_6_
  204.6 0.0 copy-start.7
  204.6 0.0 collective-permute-done.3.refs_7_
  204.6 0.8 copy-done.7
  205.4 0.0 copy-start.8
  205.4 0.7 copy-done.8
  206.1 9.0 %early.3 = (f32[8,256,256]{2,1,0:T(8,128)}, f32[8,256,128]{2,1,0:T(8,128)}) custom-call(f32[256,32,128]{2,1,0:T(8,128)} %all-to-all-done.refs_0_.refs_1_, f32[256,32,128]{2,1,0:T(8,128)} %all-to-all-done.refs_0_.refs_1_, f32[256,16,128]{2,1,0:T(8,128)} %copy-done.1, ...), custom_call_target="tpu_custom_call", output_to_operand_aliasing={{0}: (8, {}), {1}: (9, {})} | custom-call | flops 7000000000 | bytes 4194304 | tf_op jit(solution)/shard_map/early/pallas_call | solution.py:308
  215.1 0.0 copy-done.9
  215.1 0.0 copy-done.10
  215.1 23.7 %analysis.3 = f32[256,32,128]{2,1,0:T(8,128)} custom-call(f32[256,32,128]{2,1,0:T(8,128)} %all-to-all-done.refs_0_.refs_1_, f32[256,32,128]{2,1,0:T(8,128)} %all-to-all-done.refs_0_.refs_1_, f32[256,32,128]{2,1,0:T(8,128)} %all-to-all-done.1.refs_2_.refs_3_.refs_0_.refs_1_, f32[256,32,128]{2,1,0:T(8,128)} %all-to-all-done.1.refs_2_.refs_3_.refs_0_.refs_1_, ...), custom_call_target="tpu_custom_call" | custom-call | flops 24000000000 | bytes 12582912 | tf_op jit(solution)/shard_map/analysis/pallas_call | solution.py:426
  238.8 0.0 copy-start
  238.8 62.9 %all_to_all.20 = f32[256,32,128]{2,1,0:T(8,128)} all-to-all(f32[256,32,128]{2,1,0:T(8,128)} %analysis.3), channel_id=1, replica_groups=mesh['gx'=4,'gy'=32] {'gx','gy'}, dimensions={0} | all-to-all | bytes 8388608 | tf_op jit(solution)/shard_map/all_to_all | solution.py:448
  301.7 0.0 copy-done
  301.7 57.6 %all_to_all.21 = f32[256,32,128]{2,1,0:T(8,128)} all-to-all(f32[256,32,128]{2,1,0:T(8,128)S(1)} %copy-done), channel_id=1, replica_groups=mesh['gx'=4,'gy'=32] {'gx','gy'}, dimensions={0} | all-to-all | bytes 8388608 | tf_op jit(solution)/shard_map/all_to_all | solution.py:448
  359.3 9.1 %unpack.1 = f32[2,4,512,512]{3,2,1,0:T(8,128)} custom-call(f32[4,32,2,32,128]{4,3,2,1,0:T(8,128)} %bitcast.36, f32[4,32,2,32,128]{4,3,2,1,0:T(8,128)} %bitcast.35), custom_call_target="tpu_custom_call" | custom-call | tf_op jit(solution)/shard_map/unpack/pallas_call | solution.py:87
  (3 shorter events, 0.0 us)
Async XLA Ops:
  7.9 64.5 %all-to-all-start = ((f32[256,32,128]{2,1,0:T(8,128)}), f32[256,32,128]{2,1,0:T(8,128)}, u32[]{:S(2)}, u32[]{:S(2)}) async-start(f32[256,32,128]{2,1,0:T(8,128)} %bitcast.38), calls=%async_computation | async-start | bytes 8388608 | tf_op jit(solution)/shard_map/all_to_all | solution.py:448
  72.4 58.2 %all-to-all-start.1 = ((f32[256,32,128]{2,1,0:T(8,128)}), f32[256,32,128]{2,1,0:T(8,128)}, u32[]{:S(2)}, u32[]{:S(2)}) async-start(f32[256,32,128]{2,1,0:T(8,128)} %bitcast.37), calls=%async_computation.1 | async-start | bytes 8388608 | tf_op jit(solution)/shard_map/all_to_all | solution.py:448
  78.0 12.1 %copy-start.5 = (s32[1,8]{1,0:T(1,128)S(1)}, s32[1,8]{1,0:T(1,128)}, u32[]{:S(2)}) copy-start(s32[1,8]{1,0:T(1,128)} %param.9) | copy-start | bytes 100
  78.0 12.1 %copy-start.2 = (s32[1,8,1024]{2,1,0:T(8,128)S(1)}, s32[1,8,1024]{2,1,0:T(8,128)}, u32[]{:S(2)}) copy-start(s32[1,8,1024]{2,1,0:T(8,128)} %param.7) | copy-start | bytes 98308
  78.0 12.3 %copy-start.3 = (f32[1,8,1024]{2,1,0:T(8,128)S(1)}, f32[1,8,1024]{2,1,0:T(8,128)}, u32[]{:S(2)}) copy-start(f32[1,8,1024]{2,1,0:T(8,128)} %param.10) | copy-start | bytes 98308
  78.0 12.3 %copy-start.4 = (f32[1,8,1024]{2,1,0:T(8,128)S(1)}, f32[1,8,1024]{2,1,0:T(8,128)}, u32[]{:S(2)}) copy-start(f32[1,8,1024]{2,1,0:T(8,128)} %param.11) | copy-start | bytes 98308
  78.0 12.3 %copy-start.6 = (s32[1,8]{1,0:T(1,128)S(1)}, s32[1,8]{1,0:T(1,128)}, u32[]{:S(2)}) copy-start(s32[1,8]{1,0:T(1,128)} %param.8) | copy-start | bytes 100
  84.6 60.3 %collective-permute-start = (f32[256,16,128]{2,1,0:T(8,128)}, f32[256,16,128]{2,1,0:T(8,128)S(1)}, u32[]{:S(2)}, u32[]{:S(2)}) collective-permute-start(f32[256,16,128]{2,1,0:T(8,128)} %bitcast.4), channel_id=1, source_target_pairs={{0,1},{1,2},{2,3},{3,4},{4,5},{5,6},{6,7},{7,8},{8,9},{9,10},{10,1... | collective-permute-start | bytes 6291464 | tf_op jit(solution)/shard_map/ppermute | solution.py:462
  88.1 58.6 %collective-permute-start.1 = (f32[256,16,128]{2,1,0:T(8,128)}, f32[256,16,128]{2,1,0:T(8,128)}, u32[]{:S(2)}, u32[]{:S(2)}) collective-permute-start(f32[256,16,128]{2,1,0:T(8,128)} %bitcast.3), channel_id=1, source_target_pairs={{1,0},{2,1},{3,2},{4,3},{5,4},{6,5},{7,6},{8,7},{9,8},{10,9},{11,1... | collective-permute-start | bytes 6291464 | tf_op jit(solution)/shard_map/ppermute | solution.py:463
  133.2 71.3 %collective-permute-start.4 = (f32[256,128]{1,0:T(8,128)}, f32[256,128]{1,0:T(8,128)S(1)}, u32[]{:S(2)}, u32[]{:S(2)}) collective-permute-start(f32[256,128]{1,0:T(8,128)} %get-tuple-element.26), channel_id=1, source_target_pairs={{0,32},{32,64},{64,96},{96,0},{1,33},{33,65},{65,97},{97,1},{2,34}... | collective-permute-start | bytes 393224 | tf_op jit(solution)/shard_map/ppermute | solution.py:452
  133.2 71.4 %collective-permute-start.5 = (f32[256,128]{1,0:T(8,128)}, f32[256,128]{1,0:T(8,128)S(1)}, u32[]{:S(2)}, u32[]{:S(2)}) collective-permute-start(f32[256,128]{1,0:T(8,128)} %get-tuple-element.27), channel_id=1, source_target_pairs={{32,0},{64,32},{96,64},{0,96},{33,1},{65,33},{97,65},{1,97},{34,2}... | collective-permute-start | bytes 393224 | tf_op jit(solution)/shard_map/ppermute | solution.py:453
  144.9 1.8 copy-start.1
  151.6 53.0 %collective-permute-start.2 = (f32[256,256]{1,0:T(8,128)}, f32[256,256]{1,0:T(8,128)S(1)}, u32[]{:S(2)}, u32[]{:S(2)}) collective-permute-start(f32[256,256]{1,0:T(8,128)} %get-tuple-element.24), channel_id=1, source_target_pairs={{0,32},{32,64},{64,96},{96,0},{1,33},{33,65},{65,97},{97,1},{2,34}... | collective-permute-start | bytes 786440 | tf_op jit(solution)/shard_map/ppermute | solution.py:452
  153.0 51.6 %collective-permute-start.3 = (f32[256,256]{1,0:T(8,128)}, f32[256,256]{1,0:T(8,128)S(1)}, u32[]{:S(2)}, u32[]{:S(2)}) collective-permute-start(f32[256,256]{1,0:T(8,128)} %get-tuple-element.25), channel_id=1, source_target_pairs={{32,0},{64,32},{96,64},{0,96},{33,1},{65,33},{97,65},{1,97},{34,2}... | collective-permute-start | bytes 786440 | tf_op jit(solution)/shard_map/ppermute | solution.py:453
  204.6 10.5 %copy-start.9 = (f32[256,128]{1,0:T(8,128)}, f32[256,128]{1,0:T(8,128)S(1)}, u32[]{:S(2)}) copy-start(f32[256,128]{1,0:T(8,128)S(1)} %collective-permute-done.4.refs_8_) | copy-start | bytes 393220
  204.6 10.5 %copy-start.10 = (f32[256,128]{1,0:T(8,128)}, f32[256,128]{1,0:T(8,128)S(1)}, u32[]{:S(2)}) copy-start(f32[256,128]{1,0:T(8,128)S(1)} %collective-permute-done.5.refs_9_) | copy-start | bytes 393220
  204.6 0.8 copy-start.7
  205.4 0.7 copy-start.8
  238.8 62.9 %copy-start = (f32[256,32,128]{2,1,0:T(8,128)S(1)}, f32[256,32,128]{2,1,0:T(8,128)}, u32[]{:S(2)}) copy-start(f32[256,32,128]{2,1,0:T(8,128)} %analysis.2) | copy-start | bytes 12582916
where the time goes:
time: 369 us; the launch traced here: 368 us
  Pallas kernels  121 us (33%)
  blocking collectives  120 us (33%)
  waiting for transfers between devices  87.9 us (24%)
  starting transfers between devices  28.4 us (8%)
  local copies, waits for them, and re-layouts  8.06 us (2%)
    all_to_all x2, blocking collectives, exchange(): return lax.all_to_all(x, axes, split_axis=0, concat_axis=0, tiled=True)  120 us
    all_to_all x2, waiting for transfers between devices, exchange(): return lax.all_to_all(x, axes, split_axis=0, concat_axis=0, tiled=True)  77.1 us
    pallas_call x2, Pallas kernels, analysis(): pl.pallas_call(functools.partial(analysis_kernel, pairs, outer), grid=(st...  46.8 us
    pallas_call x2, Pallas kernels, early(): pl.pallas_call(functools.partial(early_kernel, start), grid=(steps,), in_...  36.1 us
    all_to_all x2, starting transfers between devices, exchange(): return lax.all_to_all(x, axes, split_axis=0, concat_axis=0, tiled=True)  17.5 us
    pallas_call x2, Pallas kernels, pack(): pl.pallas_call(functools.partial(pack_kernel, edge=edge), grid=(32 // ban...  15.8 us
    pallas_call x1, Pallas kernels, unpack(): pl.pallas_call(functools.partial(unpack_kernel, order=order), grid=(32 //...  9.12 us
    ppermute x1, waiting for transfers between devices, shards(): above = lax.ppermute(dn, 'gy', onward)  8.97 us
  transfers between devices with their start and end apart: 8, of which 4 were waited for; matrix products, arithmetic and copies ran while one was open for 2% of the time, Pallas kernels for 19%

commit v1 on v0

--- a/solution.py
+++ b/solution.py
@@ -454,13 +454,16 @@
 
     edge = exchange(pack(background, True).reshape(256, 32, 128))
     send = pack(background, False).reshape(256, 32, 128)
-    wv = cell_sums(obs_cells[0], obs_counts[0], obs_widths[0], obs_values[0], obs_variances[0])
     tiles = edge.reshape(256, 4, 8, 128)
     up = tiles[:, :, 0:4].reshape(256, 16, 128)
     dn = tiles[:, :, 4:8].reshape(256, 16, 128)
-    up, dn = lax.optimization_barrier((up, dn))
+    up, dn, obs_cells, obs_counts, obs_widths = lax.optimization_barrier(
+        (up, dn, obs_cells, obs_counts, obs_widths)
+    )
+    wv = cell_sums(obs_cells[0], obs_counts[0], obs_widths[0], obs_values[0], obs_variances[0])
     above = lax.ppermute(dn, "gy", onward)
     below = lax.ppermute(up, "gy", [(j, i) for i, j in onward])
+    send, wv = lax.optimization_barrier((send, wv))
     inner = exchange(send)
     sides_e = beside(sides(edge, ("edge", "halo"), above, below))
     partial = early(edge, above, below, wv, 0, 3)

time: 369 us -> 389 us (1.054)
  waiting for transfers between devices: 87.9 us -> 108 us
    ppermute x1, waiting for transfers between devices: 8.97 us -> 61.4 us  [shards(): above = lax.ppermute(dn, 'gy', onward)]
    all_to_all x2, waiting for transfers between devices: 77.1 us -> 44.7 us  [exchange(): return lax.all_to_all(x, axes, split_axis=0, concat_axis=0, tiled=True)]
  transfers between devices with their start and end apart: 8 -> 8, of which waited for: 4 -> 3; matrix products, arithmetic and copies ran while one was open for 2% -> 0% of each run, Pallas kernels for 19% -> 17%
where the time goes in v1:
time: 389 us; the launch traced here: 388 us
  Pallas kernels  121 us (31%)
  blocking collectives  121 us (31%)
  waiting for transfers between devices  108 us (28%)
  starting transfers between devices  28.3 us (7%)
  local copies, waits for them, and re-layouts  7.42 us (2%)
    all_to_all x2, blocking collectives, exchange(): return lax.all_to_all(x, axes, split_axis=0, concat_axis=0, tiled=True)  121 us
    ppermute x1, waiting for transfers between devices, shards(): above = lax.ppermute(dn, 'gy', onward)  61.4 us
    pallas_call x2, Pallas kernels, analysis(): pl.pallas_call(functools.partial(analysis_kernel, pairs, outer), grid=(st...  46.6 us
    all_to_all x2, waiting for transfers between devices, exchange(): return lax.all_to_all(x, axes, split_axis=0, concat_axis=0, tiled=True)  44.7 us
    pallas_call x2, Pallas kernels, early(): pl.pallas_call(functools.partial(early_kernel, start), grid=(steps,), in_...  36.2 us
    all_to_all x2, starting transfers between devices, exchange(): return lax.all_to_all(x, axes, split_axis=0, concat_axis=0, tiled=True)  17.5 us
    pallas_call x2, Pallas kernels, pack(): pl.pallas_call(functools.partial(pack_kernel, edge=edge), grid=(32 // ban...  15.8 us
    pallas_call x1, Pallas kernels, unpack(): pl.pallas_call(functools.partial(unpack_kernel, order=order), grid=(32 //...  9.12 us
  transfers between devices with their start and end apart: 8, of which 3 were waited for; matrix products, arithmetic and copies ran while one was open for 0% of the time, Pallas kernels for 17%

profile of v1, /device:TPU:1, one launch (start us, length us, event | category | flops | bytes accessed | tf_op | source)
XLA Modules:
  0.0 388.0 jit_solution(17517201239744306919)
XLA Ops:
  0.0 7.9 %pack_edge.1 = f32[4,32,2,32,128]{4,3,2,1,0:T(8,128)} custom-call(f32[2,4,512,512]{3,2,1,0:T(8,128)} %x_ref.3), custom_call_target="tpu_custom_call" | custom-call | flops 10000000000 | bytes 12582912 | tf_op jit(solution)/shard_map/pack_edge/pallas_call | solution.py:54
  7.9 11.9 %all-to-all-start = ((f32[256,32,128]{2,1,0:T(8,128)}), f32[256,32,128]{2,1,0:T(8,128)}, u32[]{:S(2)}, u32[]{:S(2)}) async-start(f32[256,32,128]{2,1,0:T(8,128)} %bitcast.38), calls=%async_computation | async-start | bytes 8388608 | tf_op jit(solution)/shard_map/all_to_all | solution.py:448
  19.9 7.9 %pack_inner.1 = f32[4,32,2,32,128]{4,3,2,1,0:T(8,128)} custom-call(f32[2,4,512,512]{3,2,1,0:T(8,128)} %x_ref.3), custom_call_target="tpu_custom_call" | custom-call | flops 10000000000 | bytes 12582912 | tf_op jit(solution)/shard_map/pack_inner/pallas_call | solution.py:54
  27.8 44.7 %all-to-all-done.refs_0_.refs_1_ = f32[256,32,128]{2,1,0:T(8,128)} async-done(((f32[256,32,128]{2,1,0:T(8,128)}), f32[256,32,128]{2,1,0:T(8,128)}, u32[]{:S(2)}, u32[]{:S(2)}) %all-to-all-start) | async-done | bytes 4194336 | tf_op jit(solution)/shard_map/all_to_all | solution.py:448
  72.4 0.0 copy-start.2
  72.4 0.0 copy-start.5
  72.4 0.0 copy-start.3
  72.4 0.0 copy-start.4
  72.5 0.0 copy-start.6
  72.5 6.6 %fusion.13 = (f32[256,4,4,128]{3,2,1,0:T(4,128)}, f32[256,4,4,128]{3,2,1,0:T(4,128)}) fusion(f32[256,4,8,128]{3,2,1,0:T(8,128)} %bitcast.2), kind=kLoop, calls=%fused_computation.39 | loop fusion | bytes 8388608 | tf_op jit(solution)/shard_map/slice | solution.py:459
  79.0 0.0 copy-done.2
  79.0 0.1 remainder_compare_fusion
  79.2 0.0 copy-done.5
  79.2 0.1 bitcast_and_fusion
  79.3 0.0 copy-done.3
  79.3 0.0 copy-done.4
  79.3 0.0 copy-done.6
  79.3 1.0 reshape_multiply_fusion
  80.3 1.3 fusion.8
  81.6 5.6 %cells.1.refs_4_.refs_5_.refs_6_.refs_7_ = f32[8,72,128]{2,1,0:T(8,128)} custom-call(s32[8,1,1024]{2,1,0:T(1,128)} %get-tuple-element.53.kc_ref, s32[8,1,1024]{2,1,0:T(1,128)} %get-tuple-element.52.lane_ref, f32[8,1,1024]{2,1,0:T(1,128)} %get-tuple-element.46.w_ref, f32[8,1,1024]{2,1,0:T(1,128)} %get-tuple-element.45.v_ref), custom_call_target="tpu_custom_call" | custom-call | flops 5000000000 | bytes 1048576 | tf_op jit(solution)/shard_map/cells/pallas_call | solution.py:156
  87.2 5.5 %all-to-all-start.1 = ((f32[256,32,128]{2,1,0:T(8,128)}), f32[256,32,128]{2,1,0:T(8,128)}, u32[]{:S(2)}, u32[]{:S(2)}) async-start(f32[256,32,128]{2,1,0:T(8,128)} %bitcast.37), calls=%async_computation.1 | async-start | bytes 8388608 | tf_op jit(solution)/shard_map/all_to_all | solution.py:448
  92.8 3.5 collective-permute-start
  96.3 1.9 collective-permute-start.1
  98.3 61.4 %collective-permute-done.refs_2_ = f32[256,16,128]{2,1,0:T(8,128)S(1)} collective-permute-done((f32[256,16,128]{2,1,0:T(8,128)}, f32[256,16,128]{2,1,0:T(8,128)S(1)}, u32[]{:S(2)}, u32[]{:S(2)}) %collective-permute-start) | collective-permute-done | bytes 2097184 | tf_op jit(solution)/shard_map/ppermute | solution.py:464
  159.7 0.0 copy-start.1
  159.7 1.8 collective-permute-done.1.refs_3_
  161.5 0.0 copy-done.1
  161.5 4.9 %sides.2 = (f32[256,256]{1,0:T(8,128)}, f32[256,256]{1,0:T(8,128)}) custom-call(f32[256,32,128]{2,1,0:T(8,128)} %all-to-all-done.refs_0_.refs_1_, f32[256,32,128]{2,1,0:T(8,128)} %all-to-all-done.refs_0_.refs_1_, f32[256,16,128]{2,1,0:T(8,128)} %copy-done.1, f32[256,16,128]{2,1,0:T(8,128)} %collective-permute-done.1.refs_3_), custom_call_target="tpu_custom_call" | custom-call | flops 1000000000 | bytes 4194304 | tf_op jit(solution)/shard_map/sides/pallas_call | solution.py:217
  166.4 1.2 collective-permute-start.2
  167.6 1.4 collective-permute-start.3
  169.1 27.1 %early.2 = (f32[8,256,256]{2,1,0:T(8,128)}, f32[8,256,128]{2,1,0:T(8,128)}) custom-call(f32[256,32,128]{2,1,0:T(8,128)} %all-to-all-done.refs_0_.refs_1_, f32[256,32,128]{2,1,0:T(8,128)} %all-to-all-done.refs_0_.refs_1_, f32[256,16,128]{2,1,0:T(8,128)} %copy-done.1, f32[256,16,128]{2,1,0:T(8,128)} %collective-permute-done.1.refs_3_, ...), custom_call_target="tpu_custom_call" | custom-call | flops 20999999488 | bytes 12582912 | tf_op jit(solution)/shard_map/early/pallas_call | solution.py:308
  196.2 0.0 all-to-all-done.1.refs_2_.refs_3_.refs_0_.refs_1_
  196.2 2.6 sides.3
  198.7 0.0 collective-permute-start.4
  198.8 2.6 collective-permute-start.5
  201.4 22.8 %analysis.2 = f32[256,32,128]{2,1,0:T(8,128)} custom-call(f32[256,32,128]{2,1,0:T(8,128)} %all-to-all-done.refs_0_.refs_1_, f32[256,32,128]{2,1,0:T(8,128)} %all-to-all-done.refs_0_.refs_1_, f32[256,32,128]{2,1,0:T(8,128)} %all-to-all-done.1.refs_2_.refs_3_.refs_0_.refs_1_, f32[256,32,128]{2,1,0:T(8,128)} %all-to-all-done.1.refs_2_.refs_3_.refs_0_.refs_1_, ...), custom_call_target="tpu_custom_call" | custom-call | flops 24000000000 | bytes 12582912 | tf_op jit(solution)/shard_map/analysis/pallas_call | solution.py:426
  224.2 0.0 collective-permute-done.2.refs_6_
  224.2 0.0 copy-start.7
  224.2 0.0 collective-permute-done.3.refs_7_
  224.3 0.0 copy-start.8
  224.3 0.0 collective-permute-done.4.refs_8_
  224.3 0.0 copy-start.9
  224.3 0.0 collective-permute-done.5.refs_9_
  224.3 0.7 copy-done.7
  225.0 0.1 copy-done.8
  225.1 0.0 copy-start.10
  225.1 9.0 %early.3 = (f32[8,256,256]{2,1,0:T(8,128)}, f32[8,256,128]{2,1,0:T(8,128)}) custom-call(f32[256,32,128]{2,1,0:T(8,128)} %all-to-all-done.refs_0_.refs_1_, f32[256,32,128]{2,1,0:T(8,128)} %all-to-all-done.refs_0_.refs_1_, f32[256,16,128]{2,1,0:T(8,128)} %copy-done.1, ...), custom_call_target="tpu_custom_call", output_to_operand_aliasing={{0}: (8, {}), {1}: (9, {})} | custom-call | flops 7000000000 | bytes 4194304 | tf_op jit(solution)/shard_map/early/pallas_call | solution.py:308
  234.2 0.0 copy-done.9
  234.2 0.0 copy-done.10
  234.2 23.7 %analysis.3 = f32[256,32,128]{2,1,0:T(8,128)} custom-call(f32[256,32,128]{2,1,0:T(8,128)} %all-to-all-done.refs_0_.refs_1_, f32[256,32,128]{2,1,0:T(8,128)} %all-to-all-done.refs_0_.refs_1_, f32[256,32,128]{2,1,0:T(8,128)} %all-to-all-done.1.refs_2_.refs_3_.refs_0_.refs_1_, f32[256,32,128]{2,1,0:T(8,128)} %all-to-all-done.1.refs_2_.refs_3_.refs_0_.refs_1_, ...), custom_call_target="tpu_custom_call" | custom-call | flops 24000000000 | bytes 12582912 | tf_op jit(solution)/shard_map/analysis/pallas_call | solution.py:426
  257.9 0.0 copy-start
  257.9 63.4 %all_to_all.20 = f32[256,32,128]{2,1,0:T(8,128)} all-to-all(f32[256,32,128]{2,1,0:T(8,128)} %analysis.3), channel_id=1, replica_groups=mesh['gx'=4,'gy'=32] {'gx','gy'}, dimensions={0} | all-to-all | bytes 8388608 | tf_op jit(solution)/shard_map/all_to_all | solution.py:448
  321.3 0.0 copy-done
  321.3 57.5 %all_to_all.21 = f32[256,32,128]{2,1,0:T(8,128)} all-to-all(f32[256,32,128]{2,1,0:T(8,128)S(1)} %copy-done), channel_id=1, replica_groups=mesh['gx'=4,'gy'=32] {'gx','gy'}, dimensions={0} | all-to-all | bytes 8388608 | tf_op jit(solution)/shard_map/all_to_all | solution.py:448
  378.9 9.1 %unpack.1 = f32[2,4,512,512]{3,2,1,0:T(8,128)} custom-call(f32[4,32,2,32,128]{4,3,2,1,0:T(8,128)} %bitcast.36, f32[4,32,2,32,128]{4,3,2,1,0:T(8,128)} %bitcast.35), custom_call_target="tpu_custom_call" | custom-call | tf_op jit(solution)/shard_map/unpack/pallas_call | solution.py:87
  (4 shorter events, 0.0 us)
Async XLA Ops:
  7.9 64.5 %all-to-all-start = ((f32[256,32,128]{2,1,0:T(8,128)}), f32[256,32,128]{2,1,0:T(8,128)}, u32[]{:S(2)}, u32[]{:S(2)}) async-start(f32[256,32,128]{2,1,0:T(8,128)} %bitcast.38), calls=%async_computation | async-start | bytes 8388608 | tf_op jit(solution)/shard_map/all_to_all | solution.py:448
  72.4 6.6 %copy-start.2 = (s32[1,8,1024]{2,1,0:T(8,128)S(1)}, s32[1,8,1024]{2,1,0:T(8,128)}, u32[]{:S(2)}) copy-start(s32[1,8,1024]{2,1,0:T(8,128)} %param.7) | copy-start | bytes 98308
  72.4 6.8 %copy-start.5 = (s32[1,8]{1,0:T(1,128)S(1)}, s32[1,8]{1,0:T(1,128)}, u32[]{:S(2)}) copy-start(s32[1,8]{1,0:T(1,128)} %param.9) | copy-start | bytes 100
  72.4 6.9 %copy-start.3 = (f32[1,8,1024]{2,1,0:T(8,128)S(1)}, f32[1,8,1024]{2,1,0:T(8,128)}, u32[]{:S(2)}) copy-start(f32[1,8,1024]{2,1,0:T(8,128)} %param.10) | copy-start | bytes 98308
  72.4 6.9 %copy-start.4 = (f32[1,8,1024]{2,1,0:T(8,128)S(1)}, f32[1,8,1024]{2,1,0:T(8,128)}, u32[]{:S(2)}) copy-start(f32[1,8,1024]{2,1,0:T(8,128)} %param.11) | copy-start | bytes 98308
  72.5 6.9 %copy-start.6 = (s32[1,8]{1,0:T(1,128)S(1)}, s32[1,8]{1,0:T(1,128)}, u32[]{:S(2)}) copy-start(s32[1,8]{1,0:T(1,128)} %param.8) | copy-start | bytes 100
  87.2 108.9 %all-to-all-start.1 = ((f32[256,32,128]{2,1,0:T(8,128)}), f32[256,32,128]{2,1,0:T(8,128)}, u32[]{:S(2)}, u32[]{:S(2)}) async-start(f32[256,32,128]{2,1,0:T(8,128)} %bitcast.37), calls=%async_computation.1 | async-start | bytes 8388608 | tf_op jit(solution)/shard_map/all_to_all | solution.py:448
  92.8 66.9 %collective-permute-start = (f32[256,16,128]{2,1,0:T(8,128)}, f32[256,16,128]{2,1,0:T(8,128)S(1)}, u32[]{:S(2)}, u32[]{:S(2)}) collective-permute-start(f32[256,16,128]{2,1,0:T(8,128)} %bitcast.40), channel_id=1, source_target_pairs={{0,1},{1,2},{2,3},{3,4},{4,5},{5,6},{6,7},{7,8},{8,9},{9,10},{10,1... | collective-permute-start | bytes 6291464 | tf_op jit(solution)/shard_map/ppermute | solution.py:464
  96.3 65.2 %collective-permute-start.1 = (f32[256,16,128]{2,1,0:T(8,128)}, f32[256,16,128]{2,1,0:T(8,128)}, u32[]{:S(2)}, u32[]{:S(2)}) collective-permute-start(f32[256,16,128]{2,1,0:T(8,128)} %bitcast.39), channel_id=1, source_target_pairs={{1,0},{2,1},{3,2},{4,3},{5,4},{6,5},{7,6},{8,7},{9,8},{10,9},{11,1... | collective-permute-start | bytes 6291464 | tf_op jit(solution)/shard_map/ppermute | solution.py:465
  159.7 1.8 copy-start.1
  166.4 57.9 %collective-permute-start.2 = (f32[256,256]{1,0:T(8,128)}, f32[256,256]{1,0:T(8,128)S(1)}, u32[]{:S(2)}, u32[]{:S(2)}) collective-permute-start(f32[256,256]{1,0:T(8,128)} %get-tuple-element.34), channel_id=1, source_target_pairs={{0,32},{32,64},{64,96},{96,0},{1,33},{33,65},{65,97},{97,1},{2,34}... | collective-permute-start | bytes 786440 | tf_op jit(solution)/shard_map/ppermute | solution.py:452
  167.6 56.6 %collective-permute-start.3 = (f32[256,256]{1,0:T(8,128)}, f32[256,256]{1,0:T(8,128)S(1)}, u32[]{:S(2)}, u32[]{:S(2)}) collective-permute-start(f32[256,256]{1,0:T(8,128)} %get-tuple-element.35), channel_id=1, source_target_pairs={{32,0},{64,32},{96,64},{0,96},{33,1},{65,33},{97,65},{1,97},{34,2}... | collective-permute-start | bytes 786440 | tf_op jit(solution)/shard_map/ppermute | solution.py:453
  198.7 25.5 %collective-permute-start.4 = (f32[256,128]{1,0:T(8,128)}, f32[256,128]{1,0:T(8,128)S(1)}, u32[]{:S(2)}, u32[]{:S(2)}) collective-permute-start(f32[256,128]{1,0:T(8,128)} %get-tuple-element.36), channel_id=1, source_target_pairs={{0,32},{32,64},{64,96},{96,0},{1,33},{33,65},{65,97},{97,1},{2,34}... | collective-permute-start | bytes 393224 | tf_op jit(solution)/shard_map/ppermute | solution.py:452
  198.8 25.5 %collective-permute-start.5 = (f32[256,128]{1,0:T(8,128)}, f32[256,128]{1,0:T(8,128)S(1)}, u32[]{:S(2)}, u32[]{:S(2)}) collective-permute-start(f32[256,128]{1,0:T(8,128)} %get-tuple-element.37), channel_id=1, source_target_pairs={{32,0},{64,32},{96,64},{0,96},{33,1},{65,33},{97,65},{1,97},{34,2}... | collective-permute-start | bytes 393224 | tf_op jit(solution)/shard_map/ppermute | solution.py:453
  224.2 0.7 copy-start.7
  224.3 0.8 copy-start.8
  224.3 9.9 %copy-start.9 = (f32[256,128]{1,0:T(8,128)}, f32[256,128]{1,0:T(8,128)S(1)}, u32[]{:S(2)}) copy-start(f32[256,128]{1,0:T(8,128)S(1)} %collective-permute-done.4.refs_8_) | copy-start | bytes 393220
  225.1 9.1 %copy-start.10 = (f32[256,128]{1,0:T(8,128)}, f32[256,128]{1,0:T(8,128)S(1)}, u32[]{:S(2)}) copy-start(f32[256,128]{1,0:T(8,128)S(1)} %collective-permute-done.5.refs_9_) | copy-start | bytes 393220
  257.9 63.4 %copy-start = (f32[256,32,128]{2,1,0:T(8,128)S(1)}, f32[256,32,128]{2,1,0:T(8,128)}, u32[]{:S(2)}) copy-start(f32[256,32,128]{2,1,0:T(8,128)} %analysis.2) | copy-start | bytes 12582916
